TPU v7x, 32 devices: a whole 2x2x4 slice. The times are simulated.
32 devices in a mesh: gx: 8 (over y, x, core), gy: 4 (over z).
Axes of the slice: x: 2, y: 2, z: 4, core: 2. Of those that a mesh axis runs over, the one named last changes fastest.
Arguments:
- rhs_conc: float32 [16, 64, 2048], P('gx', 'gy'), may hold values from -60 to 60
- rhs_pots: float32 [16, 64, 33], P('gx', 'gy'), may hold values from -60 to 60
- diffusion: float32 [16, 64, 32], P('gx', 'gy'), may hold values from 0.05 to 5
- exchange: float32 [16, 64, 32], P('gx', 'gy'), may hold values from 0.2 to 4
- slope: float32 [16, 64, 32], P('gx', 'gy'), may hold values from 0.1 to 1
Outputs:
- sol_conc: float32 [16, 64, 2048], P('gx', 'gy')
- sol_pots: float32 [16, 64, 33], P('gx', 'gy')
All inputs are finite; a program needn't handle non-finite values.
Results may differ from a plain program's by a relative error of at most 0.0003.
Values sent between devices are 32-bit elements; how exact they have to be, the bound alone decides.
No kernel may reach another device: no remote copies, remote signals or barrier semaphores. Data moves between devices by JAX's collectives and lax.ppermute only.
A program may use at most 64 MiB of HBM per device.

v0:
```python
import jax
import jax.numpy as jnp
from jax import lax
from jax.sharding import PartitionSpec as P

ITERS = 10
node_cond = 1.0
plane_cond = 0.5
collector_cond = 2.0
epsilon = 1e-06


def padded_2(cells, sides, width):
    for axis, dim in sides:
        count = lax.axis_size(axis)
        ends = count - 1
        head = lax.slice_in_dim(cells, 0, width, axis=dim)
        tail = lax.slice_in_dim(cells, cells.shape[dim] - width, cells.shape[dim], axis=dim)
        cells = jnp.concatenate(
            [
                lax.ppermute(tail, axis, [(i, (i + 1) % count) for i in range(ends)]),
                cells,
                lax.ppermute(head, axis, [((i + 1) % count, i) for i in range(ends)]),
            ],
            axis=dim,
        )
    return cells


def mirror_laplace(values):
    inner = jnp.concatenate([values[..., :1], values[..., :-1]], axis=-1)
    outer = jnp.concatenate([values[..., 1:], values[..., -1:]], axis=-1)
    return 2.0 * values - inner - outer


def local_operator(conc, padded, diffusion, exchange, slope):
    nodes = exchange.shape[2]
    shell_count = conc.shape[2] // nodes
    shells = conc.reshape(conc.shape[0], conc.shape[1], nodes, shell_count)
    center = padded[1:-1, 1:-1]
    lateral = (
        4.0 * center - padded[2:, 1:-1] - padded[:-2, 1:-1] - padded[1:-1, 2:] - padded[1:-1, :-2]
    )
    node_pot = center[..., :nodes]
    collector = center[..., nodes]
    current = exchange * (node_pot - collector[..., None])
    surface = shells[..., shell_count - 1]
    surface_flag = (lax.broadcasted_iota(jnp.int32, (shell_count,), 0) == shell_count - 1).astype(
        jnp.float32
    )
    new_shells = (
        shells + diffusion[..., None] * mirror_laplace(shells) + current[..., None] * surface_flag
    )
    new_nodes = (
        node_cond * mirror_laplace(node_pot)
        + current
        - slope * surface
        + plane_cond * lateral[..., :nodes]
    )
    new_collector = collector_cond * lateral[..., nodes] - jnp.mean(current, axis=-1)
    return (
        new_shells.reshape(conc.shape),
        jnp.concatenate([new_nodes, new_collector[..., None]], axis=-1),
    )


def least_squares(columns, start_norm):
    count = len(columns)
    target = [start_norm] + [jnp.zeros_like(start_norm) for step in range(count)]
    cosines = []
    sines = []
    upper_rows = []
    for step in range(count):
        entries = list(columns[step])
        for row in range(step):
            first = cosines[row] * entries[row] + sines[row] * entries[row + 1]
            second = cosines[row] * entries[row + 1] - sines[row] * entries[row]
            entries[row] = first
            entries[row + 1] = second
        radius = jnp.sqrt(entries[step] * entries[step] + entries[step + 1] * entries[step + 1])
        cosine = entries[step] / radius
        sine = entries[step + 1] / radius
        entries[step] = radius
        cosines.append(cosine)
        sines.append(sine)
        lead = target[step]
        target[step] = cosine * lead
        target[step + 1] = -sine * lead
        upper_rows.append(entries[: step + 1])
    weights = [None] * count
    for row in range(count - 1, -1, -1):
        total = target[row]
        for later in range(row + 1, count):
            total = total - upper_rows[later][row] * weights[later]
        weights[row] = total / upper_rows[row][row]
    return weights


def shards(rhs_conc, rhs_pots, diffusion, exchange, slope):
    local_square = jnp.sum(rhs_conc * rhs_conc) + jnp.sum(rhs_pots * rhs_pots)
    start_norm = jnp.sqrt(lax.psum(local_square, ("gx", "gy")) + epsilon)
    basis = [(rhs_conc / start_norm, rhs_pots / start_norm)]
    columns = []
    for step in range(ITERS):
        padded = padded_2(basis[step][1], (("gx", 0), ("gy", 1)), 1)
        image_conc, image_pots = local_operator(basis[step][0], padded, diffusion, exchange, slope)
        local_dots = jnp.stack(
            [jnp.sum(vector[0] * image_conc) + jnp.sum(vector[1] * image_pots) for vector in basis]
        )
        image_square = jnp.sum(image_conc * image_conc) + jnp.sum(image_pots * image_pots)
        coeffs, total_square = lax.psum((local_dots, image_square), ("gx", "gy"))
        rest_conc, rest_pots = (image_conc, image_pots)
        for row in range(step + 1):
            rest_conc = rest_conc - coeffs[row] * basis[row][0]
            rest_pots = rest_pots - coeffs[row] * basis[row][1]
        height = jnp.sqrt(total_square - jnp.sum(coeffs * coeffs) + epsilon)
        basis.append((rest_conc / height, rest_pots / height))
        columns.append([coeffs[row] for row in range(step + 1)] + [height])
    weights = least_squares(columns, start_norm)
    sol_conc = weights[0] * basis[0][0]
    sol_pots = weights[0] * basis[0][1]
    for step in range(1, ITERS):
        sol_conc = sol_conc + weights[step] * basis[step][0]
        sol_pots = sol_pots + weights[step] * basis[step][1]
    return (sol_conc, sol_pots)


def solution(mesh):
    return jax.shard_map(
        shards,
        mesh=mesh,
        in_specs=(
            P("gx", "gy", None),
            P("gx", "gy", None),
            P("gx", "gy", None),
            P("gx", "gy", None),
            P("gx", "gy", None),
        ),
        out_specs=(P("gx", "gy", None), P("gx", "gy", None)),
        check_vma=False,
    )
```

profile of v0, /device:TPU:0, one launch (start us, length us, event | category | flops | bytes accessed | tf_op | source)
XLA Modules:
  0.0 950.6 jit_solution(5201951569017878183)
XLA Ops:
  5.1 42.0 %psum.147 = f32[]{:T(128)} all-reduce(f32[]{:T(128)S(6)} %add.632), channel_id=1, replica_groups=mesh['gx'=8,'gy'=4] {'gx','gy'}, use_global_device_ids=true, to_apply=%region_2.0 | all-reduce | flops 1 | bytes 8 | tf_op jit(solution)/shard_map/psum | solution.py:101
  57.7 4.5 collective-permute-start.3
  69.2 42.0 %all-reduce.9 = (f32[]{:T(128)}, f32[1]{0:T(128)}) all-reduce(f32[]{:T(128)S(6)} %add.639, f32[1]{0:T(128)} %bitcast.3), channel_id=1, replica_groups=mesh['gx'=8,'gy'=4] {'gx','gy'}, use_global_device_ids=true, to_apply=%region_9.0 | all-reduce | flops 2 | bytes 16 | tf_op jit(solution)/shard_map/psum | solution.py:111
  124.6 4.5 collective-permute-start.7
  137.5 42.3 %all-reduce.8 = (f32[]{:T(128)}, f32[2]{0:T(128)S(1)}) all-reduce(f32[]{:T(128)S(6)} %add.649, f32[2]{0:T(128)S(1)} %pad_maximum_fusion.120), channel_id=1, replica_groups=mesh['gx'=8,'gy'=4] {'gx','gy'}, use_global_device_ids=true, to_apply=%region_18.0 | all-reduce | flops 3 | bytes 24 | tf_op jit(solution)/shard_map/psum | solution.py:111
  196.1 4.7 collective-permute-start.11
  210.8 41.6 %all-reduce.7 = (f32[]{:T(128)}, f32[3]{0:T(128)S(1)}) all-reduce(f32[]{:T(128)S(6)} %add.660, f32[3]{0:T(128)S(1)} %pad_maximum_fusion.121), channel_id=1, replica_groups=mesh['gx'=8,'gy'=4] {'gx','gy'}, use_global_device_ids=true, to_apply=%region_30.0 | all-reduce | flops 4 | bytes 32 | tf_op jit(solution)/shard_map/psum | solution.py:111
  271.7 4.5 collective-permute-start.15
  287.7 41.9 %all-reduce.6 = (f32[]{:T(128)}, f32[4]{0:T(128)S(1)}) all-reduce(f32[]{:T(128)S(6)} %add.672, f32[4]{0:T(128)S(1)} %pad_maximum_fusion.122), channel_id=1, replica_groups=mesh['gx'=8,'gy'=4] {'gx','gy'}, use_global_device_ids=true, to_apply=%region_44.0 | all-reduce | flops 5 | bytes 40 | tf_op jit(solution)/shard_map/psum | solution.py:111
  353.1 4.5 collective-permute-start.19
  370.5 41.6 %all-reduce.5 = (f32[]{:T(128)}, f32[5]{0:T(128)S(1)}) all-reduce(f32[]{:T(128)S(6)} %add.685, f32[5]{0:T(128)S(1)} %stack.210), channel_id=1, replica_groups=mesh['gx'=8,'gy'=4] {'gx','gy'}, use_global_device_ids=true, to_apply=%region_60.0 | all-reduce | flops 6 | bytes 48 | tf_op jit(solution)/shard_map/psum | solution.py:111
  438.2 4.5 collective-permute-start.23
  456.9 41.9 %all-reduce.4 = (f32[]{:T(128)}, f32[6]{0:T(128)S(1)}) all-reduce(f32[]{:T(128)S(6)} %add.699, f32[6]{0:T(128)S(1)} %stack.217), channel_id=1, replica_groups=mesh['gx'=8,'gy'=4] {'gx','gy'}, use_global_device_ids=true, to_apply=%region_78.0 | all-reduce | flops 7 | bytes 56 | tf_op jit(solution)/shard_map/psum | solution.py:111
  501.4 3.7 subtract_divide_fusion.12
  506.9 3.8 subtract_divide_fusion.3
  530.8 4.5 collective-permute-start.27
  551.5 41.6 %all-reduce.3 = (f32[]{:T(128)}, f32[7]{0:T(128)S(1)}) all-reduce(f32[]{:T(128)S(6)} %add.714, f32[7]{0:T(128)S(1)} %stack.225), channel_id=1, replica_groups=mesh['gx'=8,'gy'=4] {'gx','gy'}, use_global_device_ids=true, to_apply=%region_98.0 | all-reduce | flops 8 | bytes 64 | tf_op jit(solution)/shard_map/psum | solution.py:111
  595.8 4.4 subtract_divide_fusion.11
  602.2 4.5 subtract_divide_fusion.2
  615.2 3.6 collective-permute-start.29
  632.6 4.8 collective-permute-start.31
  659.6 40.8 %all-reduce.2 = (f32[]{:T(128)}, f32[8]{0:T(128)S(1)}) all-reduce(f32[]{:T(128)S(6)} %add.730, f32[8]{0:T(128)S(1)} %stack.234), channel_id=1, replica_groups=mesh['gx'=8,'gy'=4] {'gx','gy'}, use_global_device_ids=true, to_apply=%region_120.0 | all-reduce | flops 9 | bytes 72 | tf_op jit(solution)/shard_map/psum | solution.py:111
  703.1 5.0 subtract_divide_fusion.10
  710.7 5.1 subtract_divide_fusion.1
  726.8 3.6 collective-permute-start.33
  743.7 4.5 collective-permute-start.35
  772.0 41.0 %all-reduce.1 = (f32[]{:T(128)}, f32[9]{0:T(128)S(1)}) all-reduce(f32[]{:T(128)S(6)} %add.747, f32[9]{0:T(128)S(1)} %stack.244), channel_id=1, replica_groups=mesh['gx'=8,'gy'=4] {'gx','gy'}, use_global_device_ids=true, to_apply=%region_144.0 | all-reduce | flops 10 | bytes 80 | tf_op jit(solution)/shard_map/psum | solution.py:111
  815.7 5.7 subtract_divide_fusion.9
  824.0 6.6 subtract_divide_fusion
  843.1 3.6 collective-permute-start.37
  861.6 4.5 collective-permute-start.39
  891.7 40.8 %all-reduce = (f32[10]{0:T(128)S(1)}, f32[]{:T(128)}) all-reduce(f32[10]{0:T(128)S(1)} %stack.255, f32[]{:T(128)S(6)} %add.765), channel_id=1, replica_groups=mesh['gx'=8,'gy'=4] {'gx','gy'}, use_global_device_ids=true, to_apply=%region_167.0 | all-reduce | flops 11 | bytes 88 | tf_op jit(solution)/shard_map/psum | solution.py:111
  (524 shorter events, 226.2 us)
Async XLA Ops:
  47.9 8.4 collective-permute-start
  49.2 7.1 collective-permute-start.1
  57.7 6.5 collective-permute-start.3
  115.3 7.8 collective-permute-start.4
  116.6 6.5 collective-permute-start.5
  124.6 6.5 collective-permute-start.7
  186.2 8.4 collective-permute-start.8
  187.5 7.1 collective-permute-start.9
  196.1 6.5 collective-permute-start.11
  260.7 9.5 collective-permute-start.12
  262.0 8.2 collective-permute-start.13
  271.7 6.5 collective-permute-start.15
  340.0 11.7 %collective-permute-start.16 = (f32[1,16,33]{1,0,2:T(1,128)}, f32[1,16,33]{1,0,2:T(1,128)S(1)}, u32[]{:S(2)}, u32[]{:S(2)}) collective-permute-start(f32[1,16,33]{1,0,2:T(1,128)} %get-tuple-element.304), channel_id=1, source_target_pairs={{4,0},{8,4},{12,8},{16,12},{20,16},{24,20},{28,24},{5,1},{9,5},{13... | collective-permute-start | bytes 6344 | tf_op jit(solution)/shard_map/ppermute | solution.py:23
  341.3 10.4 %collective-permute-start.17 = (f32[1,16,33]{1,0,2:T(1,128)}, f32[1,16,33]{1,0,2:T(1,128)S(1)}, u32[]{:S(2)}, u32[]{:S(2)}) collective-permute-start(f32[1,16,33]{1,0,2:T(1,128)} %get-tuple-element.303), channel_id=1, source_target_pairs={{0,4},{4,8},{8,12},{12,16},{16,20},{20,24},{24,28},{1,5},{5,9},{9,... | collective-permute-start | bytes 6344 | tf_op jit(solution)/shard_map/ppermute | solution.py:21
  353.1 6.5 collective-permute-start.19
  423.0 13.7 %collective-permute-start.20 = (f32[1,16,33]{1,0,2:T(1,128)S(1)}, f32[1,16,33]{1,0,2:T(1,128)S(1)}, u32[]{:S(2)}, u32[]{:S(2)}) collective-permute-start(f32[1,16,33]{1,0,2:T(1,128)S(1)} %get-tuple-element.297), channel_id=1, source_target_pairs={{4,0},{8,4},{12,8},{16,12},{20,16},{24,20},{28,24},{5,1},{9,5},{13... | collective-permute-start | bytes 6344 | tf_op jit(solution)/shard_map/ppermute | solution.py:23
  424.3 12.4 %collective-permute-start.21 = (f32[1,16,33]{1,0,2:T(1,128)S(1)}, f32[1,16,33]{1,0,2:T(1,128)S(1)}, u32[]{:S(2)}, u32[]{:S(2)}) collective-permute-start(f32[1,16,33]{1,0,2:T(1,128)S(1)} %get-tuple-element.296), channel_id=1, source_target_pairs={{0,4},{4,8},{8,12},{12,16},{16,20},{20,24},{24,28},{1,5},{5,9},{9,... | collective-permute-start | bytes 6344 | tf_op jit(solution)/shard_map/ppermute | solution.py:21
  514.1 15.2 %collective-permute-start.24 = (f32[1,16,33]{1,0,2:T(1,128)}, f32[1,16,33]{1,0,2:T(1,128)S(1)}, u32[]{:S(2)}, u32[]{:S(2)}) collective-permute-start(f32[1,16,33]{1,0,2:T(1,128)} %get-tuple-element.289), channel_id=1, source_target_pairs={{4,0},{8,4},{12,8},{16,12},{20,16},{24,20},{28,24},{5,1},{9,5},{13... | collective-permute-start | bytes 6344 | tf_op jit(solution)/shard_map/ppermute | solution.py:23
  515.4 13.9 %collective-permute-start.25 = (f32[1,16,33]{1,0,2:T(1,128)}, f32[1,16,33]{1,0,2:T(1,128)S(1)}, u32[]{:S(2)}, u32[]{:S(2)}) collective-permute-start(f32[1,16,33]{1,0,2:T(1,128)} %get-tuple-element.288), channel_id=1, source_target_pairs={{0,4},{4,8},{8,12},{12,16},{16,20},{20,24},{24,28},{1,5},{5,9},{9,... | collective-permute-start | bytes 6344 | tf_op jit(solution)/shard_map/ppermute | solution.py:21
  530.8 6.5 collective-permute-start.27
  613.9 16.6 %collective-permute-start.28 = (f32[1,16,33]{1,0,2:T(1,128)}, f32[1,16,33]{1,0,2:T(1,128)S(1)}, u32[]{:S(2)}, u32[]{:S(2)}) collective-permute-start(f32[1,16,33]{1,0,2:T(1,128)} %get-tuple-element.280), channel_id=1, source_target_pairs={{4,0},{8,4},{12,8},{16,12},{20,16},{24,20},{28,24},{5,1},{9,5},{13... | collective-permute-start | bytes 6344 | tf_op jit(solution)/shard_map/ppermute | solution.py:23
  615.2 15.3 %collective-permute-start.29 = (f32[1,16,33]{1,0,2:T(1,128)}, f32[1,16,33]{1,0,2:T(1,128)}, u32[]{:S(2)}, u32[]{:S(2)}) collective-permute-start(f32[1,16,33]{1,0,2:T(1,128)} %get-tuple-element.279), channel_id=1, source_target_pairs={{0,4},{4,8},{8,12},{12,16},{16,20},{20,24},{24,28},{1,5},{5,9},{9,... | collective-permute-start | bytes 6344 | tf_op jit(solution)/shard_map/ppermute | solution.py:21
  631.3 7.2 collective-permute-start.30
  632.6 7.0 collective-permute-start.31
  725.5 16.0 %collective-permute-start.32 = (f32[1,16,33]{1,0,2:T(1,128)}, f32[1,16,33]{1,0,2:T(1,128)}, u32[]{:S(2)}, u32[]{:S(2)}) collective-permute-start(f32[1,16,33]{1,0,2:T(1,128)} %get-tuple-element.270), channel_id=1, source_target_pairs={{4,0},{8,4},{12,8},{16,12},{20,16},{24,20},{28,24},{5,1},{9,5},{13... | collective-permute-start | bytes 6344 | tf_op jit(solution)/shard_map/ppermute | solution.py:23
  726.8 14.7 %collective-permute-start.33 = (f32[1,16,33]{1,0,2:T(1,128)}, f32[1,16,33]{1,0,2:T(1,128)}, u32[]{:S(2)}, u32[]{:S(2)}) collective-permute-start(f32[1,16,33]{1,0,2:T(1,128)} %get-tuple-element.269), channel_id=1, source_target_pairs={{0,4},{4,8},{8,12},{12,16},{16,20},{20,24},{24,28},{1,5},{5,9},{9,... | collective-permute-start | bytes 6344 | tf_op jit(solution)/shard_map/ppermute | solution.py:21
  742.4 7.7 collective-permute-start.34
  743.7 7.0 collective-permute-start.35
  841.9 17.0 %collective-permute-start.36 = (f32[1,16,33]{1,0,2:T(1,128)}, f32[1,16,33]{1,0,2:T(1,128)}, u32[]{:S(2)}, u32[]{:S(2)}) collective-permute-start(f32[1,16,33]{1,0,2:T(1,128)} %get-tuple-element.259), channel_id=1, source_target_pairs={{4,0},{8,4},{12,8},{16,12},{20,16},{24,20},{28,24},{5,1},{9,5},{13... | collective-permute-start | bytes 6344 | tf_op jit(solution)/shard_map/ppermute | solution.py:23
  843.1 15.7 %collective-permute-start.37 = (f32[1,16,33]{1,0,2:T(1,128)}, f32[1,16,33]{1,0,2:T(1,128)}, u32[]{:S(2)}, u32[]{:S(2)}) collective-permute-start(f32[1,16,33]{1,0,2:T(1,128)} %get-tuple-element.258), channel_id=1, source_target_pairs={{0,4},{4,8},{8,12},{12,16},{16,20},{20,24},{24,28},{1,5},{5,9},{9,... | collective-permute-start | bytes 6344 | tf_op jit(solution)/shard_map/ppermute | solution.py:21
  860.3 7.7 collective-permute-start.38
  861.6 7.0 collective-permute-start.39
  (71 other events, 292.5 us)
where the time goes:
time: 965 us; the launch traced here: 951 us
  blocking collectives  457 us (47%)
  between operations  171 us (18%)
  other arithmetic  118 us (12%)
  starting transfers between devices  104 us (11%)
  local copies, waits for them, and re-layouts  87.2 us (9%)
  waiting for transfers between devices  12.9 us (1%)
    psum x10, blocking collectives, shards(): coeffs, total_square = lax.psum((local_dots, image_square), ('gx', 'gy'))  415 us
    ppermute x20, starting transfers between devices, padded_2(): lax.ppermute(tail, axis, [(i, (i + 1) % count) for i in range(ends)])  78.2 us
    div x18, other arithmetic, shards(): basis.append((rest_conc / height, rest_pots / height))  58.3 us
    psum x1, blocking collectives, shards(): start_norm = jnp.sqrt(lax.psum(local_square, ('gx', 'gy')) + epsilon)  42 us
    ppermute x20, starting transfers between devices, padded_2(): lax.ppermute(head, axis, [((i + 1) % count, i) for i in range(ends)])  25.8 us
  transfers between devices with their start and end apart: 40, of which 10 were waited for; matrix products, arithmetic and copies ran while one was open for 4% of the time, Pallas kernels for 0%

commit v1 on v0

--- a/solution.py
+++ b/solution.py
@@ -108,7 +108,7 @@
             [jnp.sum(vector[0] * image_conc) + jnp.sum(vector[1] * image_pots) for vector in basis]
         )
         image_square = jnp.sum(image_conc * image_conc) + jnp.sum(image_pots * image_pots)
-        coeffs, total_square = lax.psum((local_dots, image_square), ("gx", "gy"))
+        coeffs, total_square = lax.psum(lax.psum((local_dots, image_square), "gx"), "gy")
         rest_conc, rest_pots = (image_conc, image_pots)
         for row in range(step + 1):
             rest_conc = rest_conc - coeffs[row] * basis[row][0]

time: 965 us -> 793 us (0.82)
  blocking collectives: 457 us -> 283 us
    psum x10 -> x20, blocking collectives: 415 us -> 241 us  [the longest x10 126 us: shards(): lax.psum((local_dots, image_square), 'gx')]
  transfers between devices with their start and end apart: 40 -> 40, of which waited for: 10 -> 15; matrix products, arithmetic and copies ran while one was open for 4% -> 5% of each run, Pallas kernels for 0% -> 0%
where the time goes in v1:
time: 793 us; the launch traced here: 777 us
  blocking collectives  283 us (36%)
  between operations  171 us (22%)
  other arithmetic  118 us (15%)
  starting transfers between devices  104 us (13%)
  local copies, waits for them, and re-layouts  87.2 us (11%)
  waiting for transfers between devices  14.8 us (2%)
    psum x10, blocking collectives, shards(): lax.psum((local_dots, image_square), 'gx')  126 us
    psum x10, blocking collectives, shards(): lax.psum(lax.psum((local_dots, image_square), 'gx'), 'gy')  115 us
    ppermute x20, starting transfers between devices, padded_2(): lax.ppermute(tail, axis, [(i, (i + 1) % count) for i in range(ends)])  77.8 us
    div x18, other arithmetic, shards(): basis.append((rest_conc / height, rest_pots / height))  58.3 us
    psum x1, blocking collectives, shards(): start_norm = jnp.sqrt(lax.psum(local_square, ('gx', 'gy')) + epsilon)  42 us
    ppermute x20, starting transfers between devices, padded_2(): lax.ppermute(head, axis, [((i + 1) % count, i) for i in range(ends)])  25.8 us
    unnamed x139, local copies, waits for them, and re-layouts  18.5 us
  transfers between devices with their start and end apart: 40, of which 15 were waited for; matrix products, arithmetic and copies ran while one was open for 5% of the time, Pallas kernels for 0%

profile of v1, /device:TPU:0, one launch (start us, length us, event | category | flops | bytes accessed | tf_op | source)
XLA Modules:
  0.0 777.4 jit_solution(15092700923045847980)
XLA Ops:
  5.1 42.0 %psum.287 = f32[]{:T(128)} all-reduce(f32[]{:T(128)S(6)} %add.672), channel_id=1, replica_groups=mesh['gx'=8,'gy'=4] {'gx','gy'}, use_global_device_ids=true, to_apply=%region_2.0 | all-reduce | flops 1 | bytes 8 | tf_op jit(solution)/shard_map/psum | solution.py:101
  57.7 4.5 collective-permute-start.3
  69.2 13.7 %all-reduce.9 = (f32[]{:T(128)}, f32[1]{0:T(128)}) all-reduce(f32[]{:T(128)S(6)} %add.679, f32[1]{0:T(128)} %bitcast.3), channel_id=1, replica_groups=mesh['gx'=8,'gy'=4] {'gx'}, use_global_device_ids=true, to_apply=%region_10.0 | all-reduce | flops 2 | bytes 16 | tf_op jit(solution)/shard_map/psum | solution.py:111
  82.9 12.9 %all-reduce.19 = (f32[]{:T(128)}, f32[1]{0:T(128)}) all-reduce(f32[]{:T(128)} %get-tuple-element.157, f32[1]{0:T(128)} %get-tuple-element.158), channel_id=1, replica_groups=mesh['gx'=8,'gy'=4] {'gy'}, use_global_device_ids=true, to_apply=%region_11.0 | all-reduce | flops 2 | bytes 16 | tf_op jit(solution)/shard_map/psum | solution.py:111
  109.1 4.5 collective-permute-start.7
  122.3 12.4 %all-reduce.8 = (f32[]{:T(128)}, f32[2]{0:T(128)S(1)}) all-reduce(f32[]{:T(128)S(6)} %add.689, f32[2]{0:T(128)S(1)} %pad_maximum_fusion.120), channel_id=1, replica_groups=mesh['gx'=8,'gy'=4] {'gx'}, use_global_device_ids=true, to_apply=%region_21.0 | all-reduce | flops 3 | bytes 24 | tf_op jit(solution)/shard_map/psum | solution.py:111
  134.7 11.3 %all-reduce.18 = (f32[]{:T(128)}, f32[2]{0:T(128)S(1)}) all-reduce(f32[]{:T(128)} %get-tuple-element.155, f32[2]{0:T(128)S(1)} %get-tuple-element.156), channel_id=1, replica_groups=mesh['gx'=8,'gy'=4] {'gy'}, use_global_device_ids=true, to_apply=%region_22.0 | all-reduce | flops 3 | bytes 24 | tf_op jit(solution)/shard_map/psum | solution.py:111
  162.3 4.5 collective-permute-start.11
  177.6 12.4 %all-reduce.7 = (f32[]{:T(128)}, f32[3]{0:T(128)S(1)}) all-reduce(f32[]{:T(128)S(6)} %add.700, f32[3]{0:T(128)S(1)} %pad_maximum_fusion.121), channel_id=1, replica_groups=mesh['gx'=8,'gy'=4] {'gx'}, use_global_device_ids=true, to_apply=%region_35.0 | all-reduce | flops 4 | bytes 32 | tf_op jit(solution)/shard_map/psum | solution.py:111
  190.0 11.9 %all-reduce.17 = (f32[]{:T(128)}, f32[3]{0:T(128)S(1)}) all-reduce(f32[]{:T(128)} %get-tuple-element.153, f32[3]{0:T(128)S(1)} %get-tuple-element.154), channel_id=1, replica_groups=mesh['gx'=8,'gy'=4] {'gy'}, use_global_device_ids=true, to_apply=%region_36.0 | all-reduce | flops 4 | bytes 32 | tf_op jit(solution)/shard_map/psum | solution.py:111
  221.2 4.5 collective-permute-start.15
  237.8 12.4 %all-reduce.6 = (f32[]{:T(128)}, f32[4]{0:T(128)S(1)}) all-reduce(f32[]{:T(128)S(6)} %add.712, f32[4]{0:T(128)S(1)} %pad_maximum_fusion.122), channel_id=1, replica_groups=mesh['gx'=8,'gy'=4] {'gx'}, use_global_device_ids=true, to_apply=%region_51.0 | all-reduce | flops 5 | bytes 40 | tf_op jit(solution)/shard_map/psum | solution.py:111
  250.2 11.4 %all-reduce.16 = (f32[]{:T(128)}, f32[4]{0:T(128)S(1)}) all-reduce(f32[]{:T(128)} %get-tuple-element.151, f32[4]{0:T(128)S(1)} %get-tuple-element.152), channel_id=1, replica_groups=mesh['gx'=8,'gy'=4] {'gy'}, use_global_device_ids=true, to_apply=%region_52.0 | all-reduce | flops 5 | bytes 40 | tf_op jit(solution)/shard_map/psum | solution.py:111
  285.1 4.5 collective-permute-start.19
  303.1 12.4 %all-reduce.5 = (f32[]{:T(128)}, f32[5]{0:T(128)S(1)}) all-reduce(f32[]{:T(128)S(6)} %add.725, f32[5]{0:T(128)S(1)} %stack.210), channel_id=1, replica_groups=mesh['gx'=8,'gy'=4] {'gx'}, use_global_device_ids=true, to_apply=%region_69.0 | all-reduce | flops 6 | bytes 48 | tf_op jit(solution)/shard_map/psum | solution.py:111
  315.4 11.4 %all-reduce.15 = (f32[]{:T(128)}, f32[5]{0:T(128)S(1)}) all-reduce(f32[]{:T(128)} %get-tuple-element.149, f32[5]{0:T(128)S(1)} %get-tuple-element.150), channel_id=1, replica_groups=mesh['gx'=8,'gy'=4] {'gy'}, use_global_device_ids=true, to_apply=%region_70.0 | all-reduce | flops 6 | bytes 48 | tf_op jit(solution)/shard_map/psum | solution.py:111
  352.7 4.5 collective-permute-start.23
  371.9 12.4 %all-reduce.4 = (f32[]{:T(128)}, f32[6]{0:T(128)S(1)}) all-reduce(f32[]{:T(128)S(6)} %add.739, f32[6]{0:T(128)S(1)} %stack.217), channel_id=1, replica_groups=mesh['gx'=8,'gy'=4] {'gx'}, use_global_device_ids=true, to_apply=%region_89.0 | all-reduce | flops 7 | bytes 56 | tf_op jit(solution)/shard_map/psum | solution.py:111
  384.3 11.5 %all-reduce.14 = (f32[]{:T(128)}, f32[6]{0:T(128)S(1)}) all-reduce(f32[]{:T(128)} %get-tuple-element.147, f32[6]{0:T(128)S(1)} %get-tuple-element.148), channel_id=1, replica_groups=mesh['gx'=8,'gy'=4] {'gy'}, use_global_device_ids=true, to_apply=%region_90.0 | all-reduce | flops 7 | bytes 56 | tf_op jit(solution)/shard_map/psum | solution.py:111
  449.2 12.4 %all-reduce.3 = (f32[]{:T(128)}, f32[7]{0:T(128)S(1)}) all-reduce(f32[]{:T(128)S(6)} %add.754, f32[7]{0:T(128)S(1)} %stack.225), channel_id=1, replica_groups=mesh['gx'=8,'gy'=4] {'gx'}, use_global_device_ids=true, to_apply=%region_111.0 | all-reduce | flops 8 | bytes 64 | tf_op jit(solution)/shard_map/psum | solution.py:111
  461.6 11.4 %all-reduce.13 = (f32[]{:T(128)}, f32[7]{0:T(128)S(1)}) all-reduce(f32[]{:T(128)} %get-tuple-element.145, f32[7]{0:T(128)S(1)} %get-tuple-element.146), channel_id=1, replica_groups=mesh['gx'=8,'gy'=4] {'gy'}, use_global_device_ids=true, to_apply=%region_112.0 | all-reduce | flops 8 | bytes 64 | tf_op jit(solution)/shard_map/psum | solution.py:111
  539.0 12.4 %all-reduce.2 = (f32[]{:T(128)}, f32[8]{0:T(128)S(1)}) all-reduce(f32[]{:T(128)S(6)} %add.770, f32[8]{0:T(128)S(1)} %stack.234), channel_id=1, replica_groups=mesh['gx'=8,'gy'=4] {'gx'}, use_global_device_ids=true, to_apply=%region_135.0 | all-reduce | flops 9 | bytes 72 | tf_op jit(solution)/shard_map/psum | solution.py:111
  551.3 11.3 %all-reduce.12 = (f32[]{:T(128)}, f32[8]{0:T(128)S(1)}) all-reduce(f32[]{:T(128)} %get-tuple-element.143, f32[8]{0:T(128)S(1)} %get-tuple-element.144), channel_id=1, replica_groups=mesh['gx'=8,'gy'=4] {'gy'}, use_global_device_ids=true, to_apply=%region_136.0 | all-reduce | flops 9 | bytes 72 | tf_op jit(solution)/shard_map/psum | solution.py:111
  565.4 5.0 subtract_divide_fusion.10
  573.0 5.1 subtract_divide_fusion.1
  606.0 4.8 collective-permute-start.35
  634.0 13.0 %all-reduce.1 = (f32[]{:T(128)}, f32[9]{0:T(128)S(1)}) all-reduce(f32[]{:T(128)S(6)} %add.787, f32[9]{0:T(128)S(1)} %stack.244), channel_id=1, replica_groups=mesh['gx'=8,'gy'=4] {'gx'}, use_global_device_ids=true, to_apply=%region_161.0 | all-reduce | flops 10 | bytes 80 | tf_op jit(solution)/shard_map/psum | solution.py:111
  647.0 10.6 %all-reduce.11 = (f32[]{:T(128)}, f32[9]{0:T(128)S(1)}) all-reduce(f32[]{:T(128)} %get-tuple-element.141, f32[9]{0:T(128)S(1)} %get-tuple-element.142), channel_id=1, replica_groups=mesh['gx'=8,'gy'=4] {'gy'}, use_global_device_ids=true, to_apply=%region_162.0 | all-reduce | flops 10 | bytes 80 | tf_op jit(solution)/shard_map/psum | solution.py:111
  660.2 5.7 subtract_divide_fusion.9
  668.5 6.6 subtract_divide_fusion
  735.7 12.9 %all-reduce = (f32[10]{0:T(128)S(1)}, f32[]{:T(128)}) all-reduce(f32[10]{0:T(128)S(1)} %stack.255, f32[]{:T(128)S(6)} %add.805), channel_id=1, replica_groups=mesh['gx'=8,'gy'=4] {'gx'}, use_global_device_ids=true, to_apply=%region_185.0 | all-reduce | flops 11 | bytes 88 | tf_op jit(solution)/shard_map/psum | solution.py:111
  748.6 10.8 %all-reduce.10 = (f32[10]{0:T(128)S(1)}, f32[]{:T(128)}) all-reduce(f32[10]{0:T(128)S(1)} %get-tuple-element.139, f32[]{:T(128)} %get-tuple-element.140), channel_id=1, replica_groups=mesh['gx'=8,'gy'=4] {'gy'}, use_global_device_ids=true, to_apply=%region_186.0 | all-reduce | flops 11 | bytes 88 | tf_op jit(solution)/shard_map/psum | solution.py:111
  (534 shorter events, 268.8 us)
Async XLA Ops:
  47.9 8.4 %collective-permute-start = (f32[1,16,33]{1,0,2:T(1,128)S(1)}, f32[1,16,33]{1,0,2:T(1,128)S(1)}, u32[]{:S(2)}, u32[]{:S(2)}) collective-permute-start(f32[1,16,33]{1,0,2:T(1,128)S(1)} %get-tuple-element.352), channel_id=1, source_target_pairs={{4,0},{8,4},{12,8},{16,12},{20,16},{24,20},{28,24},{5,1},{9,5},{13... | collective-permute-start | bytes 6344 | tf_op jit(solution)/shard_map/ppermute | solution.py:23
  49.2 7.1 collective-permute-start.1
  99.8 7.8 collective-permute-start.4
  107.8 6.8 collective-permute-start.6
  109.1 6.7 collective-permute-start.7
  152.4 8.4 %collective-permute-start.8 = (f32[1,16,33]{1,0,2:T(1,128)S(1)}, f32[1,16,33]{1,0,2:T(1,128)S(1)}, u32[]{:S(2)}, u32[]{:S(2)}) collective-permute-start(f32[1,16,33]{1,0,2:T(1,128)S(1)} %get-tuple-element.338), channel_id=1, source_target_pairs={{4,0},{8,4},{12,8},{16,12},{20,16},{24,20},{28,24},{5,1},{9,5},{13... | collective-permute-start | bytes 6344 | tf_op jit(solution)/shard_map/ppermute | solution.py:23
  153.7 7.1 collective-permute-start.9
  162.3 7.0 collective-permute-start.11
  210.2 9.5 %collective-permute-start.12 = (f32[1,16,33]{1,0,2:T(1,128)S(1)}, f32[1,16,33]{1,0,2:T(1,128)S(1)}, u32[]{:S(2)}, u32[]{:S(2)}) collective-permute-start(f32[1,16,33]{1,0,2:T(1,128)S(1)} %get-tuple-element.331), channel_id=1, source_target_pairs={{4,0},{8,4},{12,8},{16,12},{20,16},{24,20},{28,24},{5,1},{9,5},{13... | collective-permute-start | bytes 6344 | tf_op jit(solution)/shard_map/ppermute | solution.py:23
  211.5 8.2 %collective-permute-start.13 = (f32[1,16,33]{1,0,2:T(1,128)S(1)}, f32[1,16,33]{1,0,2:T(1,128)S(1)}, u32[]{:S(2)}, u32[]{:S(2)}) collective-permute-start(f32[1,16,33]{1,0,2:T(1,128)S(1)} %get-tuple-element.330), channel_id=1, source_target_pairs={{0,4},{4,8},{8,12},{12,16},{16,20},{20,24},{24,28},{1,5},{5,9},{9,... | collective-permute-start | bytes 6344 | tf_op jit(solution)/shard_map/ppermute | solution.py:21
  219.9 6.7 collective-permute-start.14
  221.2 7.0 collective-permute-start.15
  271.9 11.7 %collective-permute-start.16 = (f32[1,16,33]{1,0,2:T(1,128)}, f32[1,16,33]{1,0,2:T(1,128)S(1)}, u32[]{:S(2)}, u32[]{:S(2)}) collective-permute-start(f32[1,16,33]{1,0,2:T(1,128)} %get-tuple-element.324), channel_id=1, source_target_pairs={{4,0},{8,4},{12,8},{16,12},{20,16},{24,20},{28,24},{5,1},{9,5},{13... | collective-permute-start | bytes 6344 | tf_op jit(solution)/shard_map/ppermute | solution.py:23
  273.2 10.4 %collective-permute-start.17 = (f32[1,16,33]{1,0,2:T(1,128)}, f32[1,16,33]{1,0,2:T(1,128)S(1)}, u32[]{:S(2)}, u32[]{:S(2)}) collective-permute-start(f32[1,16,33]{1,0,2:T(1,128)} %get-tuple-element.323), channel_id=1, source_target_pairs={{0,4},{4,8},{8,12},{12,16},{16,20},{20,24},{24,28},{1,5},{5,9},{9,... | collective-permute-start | bytes 6344 | tf_op jit(solution)/shard_map/ppermute | solution.py:21
  283.8 6.7 collective-permute-start.18
  285.1 7.0 collective-permute-start.19
  337.7 13.5 %collective-permute-start.20 = (f32[1,16,33]{1,0,2:T(1,128)S(1)}, f32[1,16,33]{1,0,2:T(1,128)S(1)}, u32[]{:S(2)}, u32[]{:S(2)}) collective-permute-start(f32[1,16,33]{1,0,2:T(1,128)S(1)} %get-tuple-element.317), channel_id=1, source_target_pairs={{4,0},{8,4},{12,8},{16,12},{20,16},{24,20},{28,24},{5,1},{9,5},{13... | collective-permute-start | bytes 6344 | tf_op jit(solution)/shard_map/ppermute | solution.py:23
  339.0 12.2 %collective-permute-start.21 = (f32[1,16,33]{1,0,2:T(1,128)S(1)}, f32[1,16,33]{1,0,2:T(1,128)S(1)}, u32[]{:S(2)}, u32[]{:S(2)}) collective-permute-start(f32[1,16,33]{1,0,2:T(1,128)S(1)} %get-tuple-element.316), channel_id=1, source_target_pairs={{0,4},{4,8},{8,12},{12,16},{16,20},{20,24},{24,28},{1,5},{5,9},{9,... | collective-permute-start | bytes 6344 | tf_op jit(solution)/shard_map/ppermute | solution.py:21
  351.4 6.7 collective-permute-start.22
  352.7 7.0 collective-permute-start.23
  411.2 15.2 %collective-permute-start.24 = (f32[1,16,33]{1,0,2:T(1,128)}, f32[1,16,33]{1,0,2:T(1,128)S(1)}, u32[]{:S(2)}, u32[]{:S(2)}) collective-permute-start(f32[1,16,33]{1,0,2:T(1,128)} %get-tuple-element.309), channel_id=1, source_target_pairs={{4,0},{8,4},{12,8},{16,12},{20,16},{24,20},{28,24},{5,1},{9,5},{13... | collective-permute-start | bytes 6344 | tf_op jit(solution)/shard_map/ppermute | solution.py:23
  412.5 13.9 %collective-permute-start.25 = (f32[1,16,33]{1,0,2:T(1,128)}, f32[1,16,33]{1,0,2:T(1,128)S(1)}, u32[]{:S(2)}, u32[]{:S(2)}) collective-permute-start(f32[1,16,33]{1,0,2:T(1,128)} %get-tuple-element.308), channel_id=1, source_target_pairs={{0,4},{4,8},{8,12},{12,16},{16,20},{20,24},{24,28},{1,5},{5,9},{9,... | collective-permute-start | bytes 6344 | tf_op jit(solution)/shard_map/ppermute | solution.py:21
  427.9 7.0 collective-permute-start.27
  493.8 16.6 %collective-permute-start.28 = (f32[1,16,33]{1,0,2:T(1,128)}, f32[1,16,33]{1,0,2:T(1,128)S(1)}, u32[]{:S(2)}, u32[]{:S(2)}) collective-permute-start(f32[1,16,33]{1,0,2:T(1,128)} %get-tuple-element.300), channel_id=1, source_target_pairs={{4,0},{8,4},{12,8},{16,12},{20,16},{24,20},{28,24},{5,1},{9,5},{13... | collective-permute-start | bytes 6344 | tf_op jit(solution)/shard_map/ppermute | solution.py:23
  495.1 15.3 %collective-permute-start.29 = (f32[1,16,33]{1,0,2:T(1,128)}, f32[1,16,33]{1,0,2:T(1,128)}, u32[]{:S(2)}, u32[]{:S(2)}) collective-permute-start(f32[1,16,33]{1,0,2:T(1,128)} %get-tuple-element.299), channel_id=1, source_target_pairs={{0,4},{4,8},{8,12},{12,16},{16,20},{20,24},{24,28},{1,5},{5,9},{9,... | collective-permute-start | bytes 6344 | tf_op jit(solution)/shard_map/ppermute | solution.py:21
  511.3 7.0 collective-permute-start.30
  587.8 16.0 %collective-permute-start.32 = (f32[1,16,33]{1,0,2:T(1,128)}, f32[1,16,33]{1,0,2:T(1,128)}, u32[]{:S(2)}, u32[]{:S(2)}) collective-permute-start(f32[1,16,33]{1,0,2:T(1,128)} %get-tuple-element.290), channel_id=1, source_target_pairs={{4,0},{8,4},{12,8},{16,12},{20,16},{24,20},{28,24},{5,1},{9,5},{13... | collective-permute-start | bytes 6344 | tf_op jit(solution)/shard_map/ppermute | solution.py:23
  589.1 14.7 %collective-permute-start.33 = (f32[1,16,33]{1,0,2:T(1,128)}, f32[1,16,33]{1,0,2:T(1,128)}, u32[]{:S(2)}, u32[]{:S(2)}) collective-permute-start(f32[1,16,33]{1,0,2:T(1,128)} %get-tuple-element.289), channel_id=1, source_target_pairs={{0,4},{4,8},{8,12},{12,16},{16,20},{20,24},{24,28},{1,5},{5,9},{9,... | collective-permute-start | bytes 6344 | tf_op jit(solution)/shard_map/ppermute | solution.py:21
  604.7 7.9 %collective-permute-start.34 = (f32[4,1,33]{1,0,2:T(4,128)S(1)}, f32[4,1,33]{1,0,2:T(4,128)S(1)}, u32[]{:S(2)}, u32[]{:S(2)}) collective-permute-start(f32[4,1,33]{1,0,2:T(4,128)S(1)} %get-tuple-element.250), channel_id=1, source_target_pairs={{1,0},{2,1},{3,2},{5,4},{6,5},{7,6},{9,8},{10,9},{11,10},{13,12},{... | collective-permute-start | bytes 1592 | tf_op jit(solution)/shard_map/ppermute | solution.py:23
  686.4 17.0 %collective-permute-start.36 = (f32[1,16,33]{1,0,2:T(1,128)}, f32[1,16,33]{1,0,2:T(1,128)}, u32[]{:S(2)}, u32[]{:S(2)}) collective-permute-start(f32[1,16,33]{1,0,2:T(1,128)} %get-tuple-element.279), channel_id=1, source_target_pairs={{4,0},{8,4},{12,8},{16,12},{20,16},{24,20},{28,24},{5,1},{9,5},{13... | collective-permute-start | bytes 6344 | tf_op jit(solution)/shard_map/ppermute | solution.py:23
  687.6 15.7 %collective-permute-start.37 = (f32[1,16,33]{1,0,2:T(1,128)}, f32[1,16,33]{1,0,2:T(1,128)}, u32[]{:S(2)}, u32[]{:S(2)}) collective-permute-start(f32[1,16,33]{1,0,2:T(1,128)} %get-tuple-element.278), channel_id=1, source_target_pairs={{0,4},{4,8},{8,12},{12,16},{16,20},{20,24},{24,28},{1,5},{5,9},{9,... | collective-permute-start | bytes 6344 | tf_op jit(solution)/shard_map/ppermute | solution.py:21
  704.8 7.7 collective-permute-start.38
  (71 other events, 277.1 us)
